TPU v7x, 32 devices: a whole 2x2x4 slice. The times are simulated.
32 devices in a mesh: row: 4 (over y, x), col: 8 (over z, core).
Axes of the slice: x: 2, y: 2, z: 4, core: 2. Of those that a mesh axis runs over, the one named last changes fastest.
Arguments:
- psi: bfloat16 [8192, 8192], P(('row', 'col')), may hold values from -0.125 to 0.125
- hpsi: bfloat16 [8192, 128], P(('row', 'col')), may hold values from -0.796875 to 0.796875
- slab_counts: int32 [32], P(('row', 'col')), may hold values from 1 to 256, 6144 in all
- matrix: float32 [4, 2048, 8, 1024], P('row', None, 'col'), as said below
Outputs:
- reduced: float32 [4, 2048, 8, 1024], P('row', None, 'col')
Inputs may be any that keep to these rules, and one draw needn't show every extreme that they name: Slab k's live plane waves are its first slab_counts[k] slots; the rest are padding; the counts sum to 3 * 256 * 32 // 4. The stored matrix is symmetric.
All inputs are finite; a program needn't handle non-finite values.
Results may differ from a plain program's by a relative error of at most 0.0003.
Values sent between devices are 32-bit elements; how exact they have to be, the bound alone decides.
No kernel may reach another device: no remote copies, remote signals or barrier semaphores. Data moves between devices by JAX's collectives and lax.ppermute only.
A program may use at most 64 MiB of HBM per device.

v0:
```python
import jax
import jax.numpy as jnp
from jax import lax
from jax.sharding import PartitionSpec as P

TILE = 16
HIGH = lax.Precision.HIGHEST


def lower_solve(factor, rhs):
    return lax.linalg.triangular_solve(factor, rhs, left_side=True, lower=True)


def invert_shifted(shifted):
    normal = jnp.dot(shifted.T, shifted, precision=HIGH)
    factor = jnp.linalg.cholesky(normal)
    first = lower_solve(factor, shifted.T)
    return lax.linalg.triangular_solve(factor, first, left_side=True, lower=True, transpose_a=True)


def per_device(psi, hpsi, slab_counts, matrix):
    prow_id = lax.axis_index("row")
    pcol_id = lax.axis_index("col")
    n_row = lax.axis_size("row")
    n_col = lax.axis_size("col")
    slots = psi.shape[0]
    panel = hpsi.shape[1]
    local_rows = matrix.shape[1]
    local_cols = matrix.shape[3]
    tiles_r = local_rows // TILE
    tiles_c = local_cols // TILE
    valid = jnp.arange(slots, dtype=jnp.int32) < slab_counts[0]
    hcols = jnp.where(valid[:, None], hpsi, jnp.zeros_like(hpsi))
    local_r = jnp.arange(local_rows, dtype=jnp.int32)
    local_c = jnp.arange(local_cols, dtype=jnp.int32)
    row_global = (local_r // TILE * n_row + prow_id) * TILE + local_r % TILE
    col_global = (local_c // TILE * n_col + pcol_id) * TILE + local_c % TILE
    partial_value = lax.dot_general(
        psi, hcols, (((0,), (0,)), ((), ())), preferred_element_type=jnp.float32
    )
    whole = lax.psum(partial_value, ("row", "col"))
    prow = lax.dynamic_index_in_dim(
        whole.reshape(tiles_r, n_row, TILE, panel), prow_id, 1, keepdims=False
    ).reshape(local_rows, panel)
    scols = lax.dynamic_index_in_dim(
        whole.reshape(tiles_c, n_col, TILE, panel), pcol_id, 1, keepdims=False
    ).reshape(local_cols, panel)
    span = jnp.arange(panel, dtype=jnp.int32)
    lower_r = jnp.where((row_global >= panel)[:, None], prow, jnp.zeros_like(prow))
    lower_c = jnp.where((col_global >= panel)[:, None], scols, jnp.zeros_like(scols))
    top_select = (row_global[None, :] == panel + span[:, None]).astype(jnp.float32)
    gram_part = jnp.dot(lower_r.T, lower_r, precision=HIGH)
    top_part = jnp.dot(top_select, prow, precision=HIGH)
    gram, top_rows = lax.psum((gram_part, top_part), "row")
    factor = jnp.linalg.cholesky(gram)
    basis_r = lower_solve(factor, lower_r.T).T
    basis_c = lower_solve(factor, lower_c.T).T
    top = lower_solve(factor, top_rows.T).T
    inverse = invert_shifted(jnp.eye(panel, dtype=jnp.float32) - top)
    embed_r = (row_global[:, None] == panel + span[None, :]).astype(jnp.float32)
    embed_c = (col_global[:, None] == panel + span[None, :]).astype(jnp.float32)
    reflect_r = basis_r - embed_r
    reflect_c = basis_c - embed_c
    stored = matrix[0, :, 0, :]
    col_select = (col_global[None, :] == span[:, None]).astype(jnp.float32)
    row_select = (row_global[None, :] == span[:, None]).astype(jnp.float32)
    left = jnp.dot(prow, col_select, precision=HIGH)
    upper = lax.dot_general(row_select, scols, (((0,), (1,)), ((), ())), precision=HIGH)
    inside_r = (row_global < panel)[:, None]
    inside_c = (col_global < panel)[None, :]
    refreshed = jnp.where(
        inside_r & inside_c,
        0.5 * (left + upper),
        jnp.where(inside_c, left, jnp.where(inside_r, upper, stored)),
    )
    zpart = jnp.dot(refreshed, reflect_c, precision=HIGH)
    zrows = lax.psum(zpart, "col")
    upart = lax.dot_general(refreshed, reflect_r, (((0,), (0,)), ((), ())), precision=HIGH)
    ucols = lax.psum(upart, "row")
    wmat = lax.psum(jnp.dot(reflect_r.T, zrows, precision=HIGH), "row")
    core = jnp.dot(jnp.dot(inverse, wmat, precision=HIGH), inverse.T, precision=HIGH)
    first = jnp.dot(reflect_r, jnp.dot(inverse, ucols.T, precision=HIGH), precision=HIGH)
    second = jnp.dot(
        jnp.dot(zrows, inverse.T, precision=HIGH) - jnp.dot(reflect_r, core, precision=HIGH),
        reflect_c.T,
        precision=HIGH,
    )
    return (refreshed - first - second)[None, :, None, :]


def solution(mesh):
    in_specs = (
        P(("row", "col"), None),
        P(("row", "col"), None),
        P(("row", "col")),
        P("row", None, "col", None),
    )
    out_specs = P("row", None, "col", None)
    return jax.shard_map(
        per_device, mesh=mesh, in_specs=in_specs, out_specs=out_specs, check_vma=False
    )
```

profile of v0, /device:TPU:0, one launch (start us, length us, event | category | flops | bytes accessed | tf_op | source)
XLA Modules:
  0.0 421.6 jit_solution(14257435263756658271)
XLA Ops:
  7.2 5.1 %convolution_bitcast_fusion = f32[8192,128]{0,1:T(8,128)} fusion(bf16[256,8192]{1,0:T(8,128)(2,1)} %param.7, bf16[256,128]{1,0:T(8,128)(2,1)} %param.8, pred[256]{0:T(512)(128)(4,1)S(1)} %iota_compare_fusion.9), kind=kOutput, calls=%fused_computation | convolution fusion | flops 536903680 | bytes 8454400 | tf_op jit(solution)/shard_map/dot_general | solution.py:38
  12.3 0.0 all-reduce.6.cloned.1.call-update
  12.3 0.0 all-reduce.8.cloned.1.call-start
  12.5 0.1 fusion.18
  12.6 145.3 %all-reduce.6.cloned.1.call-done = f32[8192,128]{0,1:T(8,128)} async-done(((f32[8192,128]{0,1:T(8,128)}), f32[8192,128]{0,1:T(8,128)}) %all-reduce.6.cloned.1.call-update) | async-done | bytes 4194320 | tf_op jit(solution)/shard_map/psum | solution.py:41
  157.9 5.6 %copy.11 = f32[8192,128]{1,0:T(8,128)} copy(f32[8192,128]{0,1:T(8,128)} %all-reduce.6.cloned.1.call-done) | data formatting | bytes 8388608 | tf_op jit(solution)/shard_map/psum | solution.py:41
  163.4 1.6 broadcast_select_fusion
  165.0 2.4 convolution_bitcast_fusion.1
  167.5 0.0 all-reduce.8.cloned.1.call-update
  167.5 0.0 all-reduce.10.cloned.1.call-start
  167.5 3.6 fusion.10
  171.1 1.3 broadcast_select_fusion.1
  172.4 11.0 %fusion.1 = f32[2048,1024]{1,0:T(8,128)} fusion(f32[2048,1024]{1,0:T(8,128)S(1)} %fusion.10, f32[1,2048,1,1024]{3,2,1,0:T(1,128)} %param.10, pred[1024]{0:T(1024)(128)(4,1)S(1)} %broadcast_compare_fusion.1, pred[2048]{0:T(1024)(128)(4,1)S(1)} %broadcast_compare_fusion, f32[1024,128]{1,0:T(8,128)S(1)} %bitcast.89, s32[2048]{0:T(1024)S(1)} %fusion.60), kind=kOutput, calls=%fused_computation.3 | convolution fusion | flops 3234332672 | bytes 25701376 | tf_op jit(solution)/shard_map/dot_general | solution.py:68
  183.3 1.6 fusion.4
  185.0 23.8 %all-reduce.8.cloned.1.call-done = f32[128,128]{0,1:T(8,128)} async-done(((f32[128,128]{0,1:T(8,128)}), f32[128,128]{0,1:T(8,128)}) %all-reduce.8.cloned.1.call-update) | async-done | bytes 65552 | tf_op jit(solution)/shard_map/psum | solution.py:54
  208.8 0.9 copy.16
  209.7 0.9 fusion.29
  210.5 11.7 %cholesky.44 = f32[128,128]{1,0:T(8,128)S(1)} custom-call(f32[128,128]{1,0:T(8,128)S(1)} %fusion.29), custom_call_target="Cholesky" | custom-call | tf_op jit(solution)/shard_map/jit(cholesky)/cholesky | solution.py:55
  222.3 0.7 compare_reduce_fusion.1
  223.0 0.7 fusion.12
  223.7 9.8 %custom-call.13 = f32[1,128,128]{1,2,0:T(8,128)S(1)} custom-call(f32[1,128,128]{2,1,0:T(8,128)S(1)} %fusion.12), custom_call_target="InvertDiagBlocksLowerTriangular" | custom-call | tf_op jit(solution)/shard_map/triangular_solve | solution.py:11
  233.5 0.6 convolution_subtract_fusion.2
  234.1 10.1 %fusion.77 = f32[2048,128]{1,0:T(8,128)} fusion(f32[2048,1024]{1,0:T(8,128)} %fusion.1, f32[1024,128]{1,0:T(8,128)S(1)} %convolution_subtract_fusion.2), kind=kOutput, calls=%fused_computation.122 | convolution fusion | flops 3221225472 | bytes 9961472 | tf_op jit(solution)/shard_map/dot_general | solution.py:76
  244.2 0.0 all-reduce.10.cloned.1.call-update
  244.2 0.0 all-reduce.12.cloned.1.call-start
  244.2 1.0 convolution_subtract_fusion.1
  245.2 16.6 %fusion.74 = f32[1024,128]{1,0:T(8,128)} fusion(f32[2048,1024]{1,0:T(8,128)} %fusion.1, f32[2048,128]{1,0:T(8,128)S(1)} %convolution_subtract_fusion.1), kind=kOutput, calls=%fused_computation.119 | convolution fusion | flops 3221225472 | bytes 9961472 | tf_op jit(solution)/shard_map/dot_general | solution.py:78
  261.8 41.8 %all-reduce.10.cloned.1.call-done = f32[2048,128]{1,0:T(8,128)} async-done(((f32[2048,128]{1,0:T(8,128)}), f32[2048,128]{1,0:T(8,128)}) %all-reduce.10.cloned.1.call-update) | async-done | bytes 1048592 | tf_op jit(solution)/shard_map/psum | solution.py:77
  303.7 3.7 fusion.79
  307.3 0.0 all-reduce.12.cloned.1.call-update
  307.3 46.2 %all-reduce.12.cloned.1.call-done = (f32[128,128]{1,0:T(8,128)}, f32[1024,128]{1,0:T(8,128)}, f32[128,128]{1,0:T(8,128)}) async-done(((f32[128,128]{1,0:T(8,128)}, f32[1024,128]{1,0:T(8,128)}, f32[128,128]{1,0:T(8,128)}), (f32[128,128]{1,0:T(8,128)}, f32[1024,128]{1,0:T(8,128)}, f32[128,128]{1,0:T(8,128)})) %all-reduce.12.cloned.1.call-update) | async-done | bytes 655376 | tf_op jit(solution)/shard_map/psum | solution.py:54
  353.6 1.1 fusion.25
  354.7 0.3 fusion.24
  355.0 0.1 copy.17
  355.1 11.7 %cholesky.55 = f32[128,128]{1,0:T(8,128)S(1)} custom-call(f32[128,128]{1,0:T(8,128)S(1)} %fusion.23), custom_call_target="Cholesky" | custom-call | tf_op jit(solution)/shard_map/jit(cholesky)/cholesky | solution.py:16
  366.8 0.6 compare_reduce_fusion
  367.4 0.6 fusion.13
  368.0 9.8 %custom-call.14 = f32[1,128,128]{1,2,0:T(8,128)S(1)} custom-call(f32[1,128,128]{2,1,0:T(8,128)S(1)} %fusion.13), custom_call_target="InvertDiagBlocksLowerTriangular" | custom-call | tf_op jit(solution)/shard_map/triangular_solve | solution.py:18
  377.8 0.3 fusion.19
  378.1 0.2 fusion.21
  378.3 1.0 fusion.80
  379.4 0.3 fusion.81
  379.7 1.8 fusion.75
  381.4 7.2 %fusion.76 = f32[2048,1024]{1,0:T(8,128)S(1)} fusion(f32[2048,128]{1,0:T(8,128)S(1)} %convolution_subtract_fusion.1, f32[128,1024]{1,0:T(8,128)S(1)} %fusion.75), kind=kOutput, calls=%fused_computation.121 | convolution fusion | flops 3221225472 | bytes 9961472 | tf_op jit(solution)/shard_map/dot_general | solution.py:82
  388.7 1.0 fusion.78
  389.7 1.0 convolution_subtract_fusion
  390.7 8.0 %subtract_bitcast_fusion = f32[1,2048,1,1024]{3,1,2,0:T(8,128)S(1)} fusion(f32[2048,1024]{1,0:T(8,128)S(1)} %bitcast.83, f32[2048,1024]{1,0:T(8,128)S(1)} %fusion.76, f32[2048,128]{1,0:T(8,128)S(1)} %convolution_subtract_fusion, f32[1024,128]{1,0:T(8,128)S(1)} %convolution_subtract_fusion.2), kind=kOutput, calls=%fused_computation.4 | convolution fusion | flops 3225419776 | bytes 26738688 | tf_op jit(solution)/shard_map/dot_general | solution.py:83
  398.7 16.1 %copy.18 = f32[1,2048,1,1024]{3,2,1,0:T(1,128)} copy(f32[1,2048,1,1024]{3,1,2,0:T(8,128)S(1)} %subtract_bitcast_fusion) | data formatting | bytes 16777216 | tf_op jit(solution)/shard_map/broadcast_in_dim | solution.py:88
  (18 shorter events, 0.2 us)
Async XLA Ops:
  6.5 151.3 %all-reduce.6.cloned.1.call-start = ((), (), s32[]{:S(2)}) async-start(), calls=%async_computation | async-start | bytes 8388608 | tf_op jit(solution)/shard_map/psum | solution.py:41
  12.3 196.4 %all-reduce.8.cloned.1.call-start = ((), (), s32[]{:S(2)}) async-start(), calls=%async_computation.1 | async-start | bytes 131072 | tf_op jit(solution)/shard_map/psum | solution.py:54
  167.5 136.2 %all-reduce.10.cloned.1.call-start = ((), (), s32[]{:S(2)}) async-start(), calls=%async_computation.2 | async-start | bytes 2097152 | tf_op jit(solution)/shard_map/psum | solution.py:77
  244.2 109.4 %all-reduce.12.cloned.1.call-start = ((), (), s32[]{:S(2)}) async-start(), calls=%async_computation.3 | async-start | bytes 1310720 | tf_op jit(solution)/shard_map/psum | solution.py:54
  379.6 9.0 %copy-start = (f32[2048,128]{1,0:T(8,128)S(1)}, f32[2048,128]{1,0:T(8,128)}, u32[]{:S(2)}) copy-start(f32[2048,128]{1,0:T(8,128)} %all-reduce.10.cloned.1.call-done) | copy-start | bytes 3145732
  379.6 11.0 %slice-start = ((s8[8388608]{0:T(1024)(128)(4,1)}), s8[4194304]{0:T(1024)(128)(4,1)S(1)}, s32[]{:S(2)}) async-start(s8[8388608]{0:T(1024)(128)(4,1)} %bitcast.82), calls=%async_computation.4 | async-start | bytes 8388608
  381.4 9.3 %slice-start.1 = ((s8[8388608]{0:T(1024)(128)(4,1)}), s8[4194304]{0:T(1024)(128)(4,1)S(1)}, s32[]{:S(2)}) async-start(s8[8388608]{0:T(1024)(128)(4,1)} %bitcast.82), calls=%async_computation.5 | async-start | bytes 8388608
Sparse Core Ops, SparseCore 0:
  12.9 144.9 all-reduce.5
  167.6 41.1 all-reduce.7
  244.3 59.2 all-reduce.9
  307.5 46.0 all-reduce.11
where the time goes:
time: 428 us; the launch traced here: 422 us
  waiting for transfers between devices  257 us (60%)
  matrix products  77.7 us (18%)
  other arithmetic  49.6 us (12%)
  local copies, waits for them, and re-layouts  22.7 us (5%)
  between operations  14.3 us (3%)
    psum x1, waiting for transfers between devices, per_device(): whole = lax.psum(partial_value, ('row', 'col'))  145 us
    psum x2, waiting for transfers between devices, per_device(): gram, top_rows = lax.psum((gram_part, top_part), 'row')  70 us
    psum x1, waiting for transfers between devices, per_device(): zrows = lax.psum(zpart, 'col')  41.8 us
    dot_general x1, matrix products, per_device(): lax.dot_general(refreshed, reflect_r, (((0,), (0,)), ((), ())), precision...  16.6 us
    broadcast_in_dim x1, local copies, waits for them, and re-layouts, per_device(): return (refreshed - first - second)[None, :, None, :]  16.1 us
    another operation x3, other arithmetic, per_device(): factor = jnp.linalg.cholesky(gram)  12.5 us
    another operation x3, other arithmetic, invert_shifted(): factor = jnp.linalg.cholesky(normal)  12.4 us
    dot_general x1, matrix products, per_device(): lax.dot_general(row_select, scols, (((0,), (1,)), ((), ())), precision=HIGH)  11 us
  transfers between devices with their start and end apart: 4, of which 4 were waited for; matrix products, arithmetic and copies ran while one was open for 8% of the time, Pallas kernels for 0%

commit v1 on v0

--- a/solution.py
+++ b/solution.py
@@ -74,7 +74,9 @@
         jnp.where(inside_c, left, jnp.where(inside_r, upper, stored)),
     )
     zpart = jnp.dot(refreshed, reflect_c, precision=HIGH)
-    zrows = lax.psum(zpart, "col")
+    zrows = zpart
+    for hop in (1, 2, 4):
+        zrows = zrows + lax.ppermute(zrows, "col", [(dev, dev ^ hop) for dev in range(8)])
     upart = lax.dot_general(refreshed, reflect_r, (((0,), (0,)), ((), ())), precision=HIGH)
     ucols = lax.psum(upart, "row")
     wmat = lax.psum(jnp.dot(reflect_r.T, zrows, precision=HIGH), "row")

time: 428 us -> 446 us (1.042)
  waiting for transfers between devices: 257 us -> 273 us
    ppermute x0 -> x3, waiting for transfers between devices: none -> 54.5 us  [per_device(): lax.ppermute(zrows, 'col', [(dev, dev ^ hop) for dev in range(8)])]
    psum x1 -> x0, waiting for transfers between devices: 41.8 us -> none  [per_device(): zrows = lax.psum(zpart, 'col')]
  transfers between devices with their start and end apart: 4 -> 6, of which waited for: 4 -> 6; matrix products, arithmetic and copies ran while one was open for 8% -> 8% of each run, Pallas kernels for 0% -> 0%
where the time goes in v1:
time: 446 us; the launch traced here: 440 us
  waiting for transfers between devices  273 us (61%)
  matrix products  74.8 us (17%)
  other arithmetic  49.8 us (11%)
  local copies, waits for them, and re-layouts  23.7 us (5%)
  between operations  14.6 us (3%)
    psum x1, waiting for transfers between devices, per_device(): whole = lax.psum(partial_value, ('row', 'col'))  146 us
    psum x2, waiting for transfers between devices, per_device(): gram, top_rows = lax.psum((gram_part, top_part), 'row')  72.5 us
    ppermute x3, waiting for transfers between devices, per_device(): lax.ppermute(zrows, 'col', [(dev, dev ^ hop) for dev in range(8)])  54.5 us
    broadcast_in_dim x1, local copies, waits for them, and re-layouts, per_device(): return (refreshed - first - second)[None, :, None, :]  16.1 us
    dot_general x1, matrix products, per_device(): lax.dot_general(refreshed, reflect_r, (((0,), (0,)), ((), ())), precision...  14.5 us
    another operation x3, other arithmetic, invert_shifted(): factor = jnp.linalg.cholesky(normal)  12.5 us
    another operation x3, other arithmetic, per_device(): factor = jnp.linalg.cholesky(gram)  12.4 us
    dot_general x1, matrix products, per_device(): lax.dot_general(row_select, scols, (((0,), (1,)), ((), ())), precision=HIGH)  11 us
  transfers between devices with their start and end apart: 6, of which 6 were waited for; matrix products, arithmetic and copies ran while one was open for 8% of the time, Pallas kernels for 0%

profile of v1, /device:TPU:0, one launch (start us, length us, event | category | flops | bytes accessed | tf_op | source)
XLA Modules:
  0.0 439.7 jit_solution(13282865287849169796)
XLA Ops:
  7.2 5.1 %convolution_bitcast_fusion = f32[8192,128]{0,1:T(8,128)} fusion(bf16[256,8192]{1,0:T(8,128)(2,1)} %param.7, bf16[256,128]{1,0:T(8,128)(2,1)} %param.8, pred[256]{0:T(512)(128)(4,1)S(1)} %iota_compare_fusion.9), kind=kOutput, calls=%fused_computation | convolution fusion | flops 536903680 | bytes 8454400 | tf_op jit(solution)/shard_map/dot_general | solution.py:38
  12.5 0.1 fusion.21
  12.6 145.6 %all-reduce.5.cloned.1.call-done = f32[8192,128]{0,1:T(8,128)} async-done(((f32[8192,128]{0,1:T(8,128)}), f32[8192,128]{0,1:T(8,128)}) %all-reduce.5.cloned.1.call-update) | async-done | bytes 4194320 | tf_op jit(solution)/shard_map/psum | solution.py:41
  158.2 5.6 %copy.11 = f32[8192,128]{1,0:T(8,128)} copy(f32[8192,128]{0,1:T(8,128)} %all-reduce.5.cloned.1.call-done) | data formatting | bytes 8388608 | tf_op jit(solution)/shard_map/psum | solution.py:41
  163.7 1.6 broadcast_select_fusion
  165.3 2.4 convolution_bitcast_fusion.1
  167.8 3.6 fusion.10
  171.4 1.3 broadcast_select_fusion.1
  172.7 11.0 %fusion.1 = f32[2048,1024]{1,0:T(8,128)} fusion(f32[2048,1024]{1,0:T(8,128)S(1)} %fusion.10, f32[1,2048,1,1024]{3,2,1,0:T(1,128)} %param.10, pred[1024]{0:T(1024)(128)(4,1)S(1)} %broadcast_compare_fusion.1, pred[2048]{0:T(1024)(128)(4,1)S(1)} %broadcast_compare_fusion, f32[1024,128]{1,0:T(8,128)S(1)} %bitcast.89, s32[2048]{0:T(1024)S(1)} %fusion.63), kind=kOutput, calls=%fused_computation.3 | convolution fusion | flops 3234332672 | bytes 25701376 | tf_op jit(solution)/shard_map/dot_general | solution.py:68
  183.7 25.3 %all-reduce.7.cloned.1.call-done = f32[128,128]{0,1:T(8,128)} async-done(((f32[128,128]{0,1:T(8,128)}), f32[128,128]{0,1:T(8,128)}) %all-reduce.7.cloned.1.call-update) | async-done | bytes 65552 | tf_op jit(solution)/shard_map/psum | solution.py:54
  209.0 0.9 copy.16
  210.0 0.9 fusion.32
  210.8 11.7 %cholesky.44 = f32[128,128]{1,0:T(8,128)S(1)} custom-call(f32[128,128]{1,0:T(8,128)S(1)} %fusion.32), custom_call_target="Cholesky" | custom-call | tf_op jit(solution)/shard_map/jit(cholesky)/cholesky | solution.py:55
  222.6 0.6 compare_reduce_fusion.1
  223.2 0.6 fusion.15
  223.8 9.8 %custom-call.13 = f32[1,128,128]{1,2,0:T(8,128)S(1)} custom-call(f32[1,128,128]{2,1,0:T(8,128)S(1)} %fusion.15), custom_call_target="InvertDiagBlocksLowerTriangular" | custom-call | tf_op jit(solution)/shard_map/triangular_solve | solution.py:11
  233.6 0.6 convolution_subtract_fusion.2
  234.2 10.5 %fusion.80 = f32[2048,128]{1,0:T(8,128)S(1)} fusion(f32[2048,1024]{1,0:T(8,128)} %fusion.1, f32[1024,128]{1,0:T(8,128)S(1)} %convolution_subtract_fusion.2), kind=kOutput, calls=%fused_computation.125 | convolution fusion | flops 3221225472 | bytes 9961472 | tf_op jit(solution)/shard_map/dot_general | solution.py:76
  244.8 2.6 collective-permute-done
  247.4 0.1 add.252
  247.5 1.6 collective-permute-start.1
  249.1 23.7 %collective-permute-done.1 = f32[2048,128]{1,0:T(8,128)S(1)} collective-permute-done((f32[2048,128]{1,0:T(8,128)S(1)}, f32[2048,128]{1,0:T(8,128)S(1)}, u32[]{:S(2)}, u32[]{:S(2)}) %collective-permute-start.1) | collective-permute-done | bytes 1048608 | tf_op jit(solution)/shard_map/ppermute | solution.py:79
  272.8 0.1 add.253
  272.9 2.5 collective-permute-start.2
  275.4 1.7 fusion.4
  277.0 1.0 convolution_subtract_fusion.1
  278.0 14.5 %fusion.77 = f32[1024,128]{1,0:T(8,128)} fusion(f32[2048,1024]{1,0:T(8,128)S(1)} %bitcast.81, f32[2048,128]{1,0:T(8,128)S(1)} %convolution_subtract_fusion.1), kind=kOutput, calls=%fused_computation.122 | convolution fusion | flops 3221225472 | bytes 9961472 | tf_op jit(solution)/shard_map/dot_general | solution.py:80
  292.5 28.1 %collective-permute-done.2 = f32[2048,128]{1,0:T(8,128)S(1)} collective-permute-done((f32[2048,128]{1,0:T(8,128)S(1)}, f32[2048,128]{1,0:T(8,128)S(1)}, u32[]{:S(2)}, u32[]{:S(2)}) %collective-permute-start.2) | collective-permute-done | bytes 1048608 | tf_op jit(solution)/shard_map/ppermute | solution.py:79
  320.7 1.0 copy-done.2
  321.6 2.5 fusion.11
  324.1 47.1 %all-reduce.9.cloned.1.call-done = (f32[128,128]{1,0:T(8,128)}, f32[1024,128]{1,0:T(8,128)}, f32[128,128]{1,0:T(8,128)}) async-done(((f32[128,128]{1,0:T(8,128)}, f32[1024,128]{1,0:T(8,128)}, f32[128,128]{1,0:T(8,128)}), (f32[128,128]{1,0:T(8,128)}, f32[1024,128]{1,0:T(8,128)}, f32[128,128]{1,0:T(8,128)})) %all-reduce.9.cloned.1.call-update) | async-done | bytes 655376 | tf_op jit(solution)/shard_map/psum | solution.py:54
  371.3 1.1 fusion.28
  372.4 0.3 fusion.27
  372.7 0.1 copy.17
  372.8 11.7 %cholesky.55 = f32[128,128]{1,0:T(8,128)S(1)} custom-call(f32[128,128]{1,0:T(8,128)S(1)} %fusion.26), custom_call_target="Cholesky" | custom-call | tf_op jit(solution)/shard_map/jit(cholesky)/cholesky | solution.py:16
  384.5 0.7 compare_reduce_fusion
  385.2 0.7 fusion.16
  385.9 9.8 %custom-call.14 = f32[1,128,128]{1,2,0:T(8,128)S(1)} custom-call(f32[1,128,128]{2,1,0:T(8,128)S(1)} %fusion.16), custom_call_target="InvertDiagBlocksLowerTriangular" | custom-call | tf_op jit(solution)/shard_map/triangular_solve | solution.py:18
  395.8 0.3 fusion.22
  396.1 0.2 fusion.24
  396.3 1.0 fusion.81
  397.3 0.3 fusion.82
  397.6 1.9 fusion.78
  399.5 1.0 fusion.83
  400.5 7.0 %fusion.79 = f32[2048,1024]{1,0:T(8,128)S(1)} fusion(f32[2048,128]{1,0:T(8,128)S(1)} %convolution_subtract_fusion.1, f32[128,1024]{1,0:T(8,128)S(1)} %fusion.78), kind=kOutput, calls=%fused_computation.124 | convolution fusion | flops 3221225472 | bytes 9961472 | tf_op jit(solution)/shard_map/dot_general | solution.py:84
  407.5 1.0 convolution_subtract_fusion
  408.6 8.0 %subtract_bitcast_fusion = f32[1,2048,1,1024]{3,1,2,0:T(8,128)S(1)} fusion(f32[2048,1024]{1,0:T(8,128)S(1)} %bitcast.83, f32[2048,1024]{1,0:T(8,128)S(1)} %fusion.79, f32[2048,128]{1,0:T(8,128)S(1)} %convolution_subtract_fusion, f32[1024,128]{1,0:T(8,128)S(1)} %copy-done.1), kind=kOutput, calls=%fused_computation.4 | convolution fusion | flops 3225419776 | bytes 26738688 | tf_op jit(solution)/shard_map/dot_general | solution.py:85
  416.6 16.1 %copy.18 = f32[1,2048,1,1024]{3,2,1,0:T(1,128)} copy(f32[1,2048,1,1024]{3,1,2,0:T(8,128)S(1)} %subtract_bitcast_fusion) | data formatting | bytes 16777216 | tf_op jit(solution)/shard_map/broadcast_in_dim | solution.py:90
  (34 shorter events, 0.4 us)
Async XLA Ops:
  6.5 151.6 %all-reduce.5.cloned.1.call-start = ((), (), s32[]{:S(2)}) async-start(), calls=%async_computation | async-start | bytes 8388608 | tf_op jit(solution)/shard_map/psum | solution.py:41
  12.3 196.7 %all-reduce.7.cloned.1.call-start = ((), (), s32[]{:S(2)}) async-start(), calls=%async_computation.1 | async-start | bytes 131072 | tf_op jit(solution)/shard_map/psum | solution.py:54
  167.8 203.5 %all-reduce.9.cloned.1.call-start = ((), (), s32[]{:S(2)}) async-start(), calls=%async_computation.2 | async-start | bytes 1310720 | tf_op jit(solution)/shard_map/psum | solution.py:54
  233.6 44.4 %slice-start = ((s8[8388608]{0:T(1024)(128)(4,1)}), s8[4194304]{0:T(1024)(128)(4,1)S(1)}, s32[]{:S(2)}) async-start(s8[8388608]{0:T(1024)(128)(4,1)} %bitcast.80), calls=%async_computation.3 | async-start | bytes 8388608
  234.2 42.9 %copy-start = (f32[1024,128]{1,0:T(8,128)}, f32[1024,128]{1,0:T(8,128)S(1)}, u32[]{:S(2)}) copy-start(f32[1024,128]{1,0:T(8,128)S(1)} %convolution_subtract_fusion.2) | copy-start | bytes 1572868
  234.2 43.8 %slice-start.1 = ((s8[8388608]{0:T(1024)(128)(4,1)}), s8[4194304]{0:T(1024)(128)(4,1)S(1)}, s32[]{:S(2)}) async-start(s8[8388608]{0:T(1024)(128)(4,1)} %bitcast.80), calls=%async_computation.4 | async-start | bytes 8388608
  244.7 2.7 collective-permute-start
  247.5 25.3 %collective-permute-start.1 = (f32[2048,128]{1,0:T(8,128)S(1)}, f32[2048,128]{1,0:T(8,128)S(1)}, u32[]{:S(2)}, u32[]{:S(2)}) collective-permute-start(f32[2048,128]{1,0:T(8,128)S(1)} %add.252), channel_id=1, source_target_pairs={{0,2},{1,3},{2,0},{3,1},{4,6},{5,7},{6,4},{7,5},{8,10},{9,11},{10,... | collective-permute-start | bytes 3145736 | tf_op jit(solution)/shard_map/ppermute | solution.py:79
  272.9 47.8 %collective-permute-start.2 = (f32[2048,128]{1,0:T(8,128)S(1)}, f32[2048,128]{1,0:T(8,128)S(1)}, u32[]{:S(2)}, u32[]{:S(2)}) collective-permute-start(f32[2048,128]{1,0:T(8,128)S(1)} %add.253), channel_id=1, source_target_pairs={{0,4},{1,5},{2,6},{3,7},{4,0},{5,1},{6,2},{7,3},{8,12},{9,13},{10,... | collective-permute-start | bytes 3145736 | tf_op jit(solution)/shard_map/ppermute | solution.py:79
  320.7 1.0 copy-start.2
  399.4 9.1 %slice-start.2 = ((s8[8388608]{0:T(1024)(128)(4,1)}), s8[4194304]{0:T(1024)(128)(4,1)S(1)}, s32[]{:S(2)}) async-start(s8[8388608]{0:T(1024)(128)(4,1)} %bitcast.82), calls=%async_computation.5 | async-start | bytes 8388608
  400.4 7.1 %copy-start.3 = (f32[2048,128]{1,0:T(8,128)S(1)}, f32[2048,128]{1,0:T(8,128)}, u32[]{:S(2)}) copy-start(f32[2048,128]{1,0:T(8,128)} %copy-done.2) | copy-start | bytes 3145732
  400.4 8.1 %slice-start.3 = ((s8[8388608]{0:T(1024)(128)(4,1)}), s8[4194304]{0:T(1024)(128)(4,1)S(1)}, s32[]{:S(2)}) async-start(s8[8388608]{0:T(1024)(128)(4,1)} %bitcast.82), calls=%async_computation.6 | async-start | bytes 8388608
  400.5 8.1 %copy-start.1 = (f32[1024,128]{1,0:T(8,128)S(1)}, f32[1024,128]{1,0:T(8,128)}, u32[]{:S(2)}) copy-start(f32[1024,128]{1,0:T(8,128)} %copy-done) | copy-start | bytes 1572868
Sparse Core Ops, SparseCore 0:
  12.9 145.2 all-reduce.4
  167.9 41.0 all-reduce.6
  324.3 46.9 all-reduce.8
